TPU v7x, 32 devices: a whole 2x2x4 slice. The times are simulated.
32 devices in a mesh: section: 4 (over y, x), tp: 8 (over z, core).
Axes of the slice: x: 2, y: 2, z: 4, core: 2. Of those that a mesh axis runs over, the one named last changes fastest.
Arguments:
- awaiting_arrivals: bfloat16 [4, 8, 25, 1920], P('section', 'tp'), may hold values from -6 to 6
- label_numbers: int32 [5, 8], replicated, may hold values from 0 to 1000
- drawn_coarse_codes: int32 [1, 8, 30], replicated, may hold values from 0 to 4095
- discrete_prototypes: float32 [4096, 32], replicated, may hold values from -6 to 6
- code_raising_operator: bfloat16 [32, 1920], replicated, may hold values from -1 to 1
- placement_tier_features: bfloat16 [25, 1920], replicated, may hold values from -3 to 3
- label_feature_rows: bfloat16 [1001, 1920], P(None, 'tp'), may hold values from -6 to 6
- conditioned_gain_mapping: bfloat16 [4, 1920, 3, 1920], P('section', None, None, 'tp'), may hold values from -0.125 to 0.125
- conditioned_shift_addend: float32 [4, 3, 1920], P('section', None, 'tp'), may hold values from -3 to 3
- question_answer_operator: bfloat16 [4, 1920, 3, 1920], P('section', None, None, 'tp'), may hold values from -0.125 to 0.125
- mixing_return_operator: bfloat16 [4, 1920, 1920], P('section', None, 'tp'), may hold values from -0.125 to 0.125
- focus_sharpness_exponents: float32 [4, 30], P('section'), may hold values from 1 to 5.5
- prior_resolution_probes: bfloat16 [4, 2, 8, 30, 1920], P('section', None, 'tp'), may hold values from -0.75 to 0.75
- prior_resolution_answers: bfloat16 [4, 2, 8, 30, 1920], P('section', None, 'tp'), may hold values from -6 to 6
Outputs:
- section_out: bfloat16 [4, 2, 8, 25, 1920], P('section', None, 'tp')
Inputs may be any that keep to these rules, and one draw needn't show every extreme that they name: `drawn_coarse_codes`: codebook indices of the maps of sides 1 to 4 of each image, one map after another, each row by row. `label_numbers`: class of each image; row r belongs to the micro-batch r - 4.
All inputs are finite; a program needn't handle non-finite values.
Results may differ from a plain program's by a relative error of at most 0.0151.
Values may be sent and summed in bfloat16 or wider, within the bound.
No kernel may reach another device: no remote copies, remote signals or barrier semaphores. Data moves between devices by JAX's collectives and lax.ppermute only.
A program may use at most 128 MiB of HBM per device.

v0:
```python
import jax
import jax.numpy as jnp
from jax import lax
from jax.sharding import PartitionSpec as P

FOCUS_GROUPS = 30
HEAD_DIM = 64
SIDE = 5
LOG_CAP = 4.605170185988092


def shifted(value, axis, steps):
    count = lax.axis_size(axis)
    first, last = (max(0, -steps), min(count, count - steps))
    return lax.ppermute(value, axis, [(source, source + steps) for source in range(first, last)])


def crossing_matrix(target, coarse):
    fine_index = jnp.arange(target, dtype=jnp.float32)
    coarse_index = jnp.arange(coarse, dtype=jnp.float32)
    begins = jnp.maximum(fine_index[:, None] / target, coarse_index[None, :] / coarse)
    finish = jnp.minimum(
        (fine_index[:, None] + 1.0) / target, (coarse_index[None, :] + 1.0) / coarse
    )
    return jnp.maximum(finish - begins, 0.0) * target


def resampler():
    blocks = []
    for coarse in range(1, SIDE):
        crossing = crossing_matrix(SIDE, coarse)
        blocks.append(
            (crossing[:, None, :, None] * crossing[None, :, None, :]).reshape(
                SIDE * SIDE, coarse * coarse
            )
        )
    return jnp.concatenate(blocks, axis=1)


def embed(
    drawn_coarse_codes,
    discrete_prototypes,
    code_raising_operator,
    placement_tier_features,
    resample_table,
):
    looked_up = discrete_prototypes[drawn_coarse_codes]
    mapped = jnp.einsum(
        "tc,nicv->nitv", resample_table, looked_up, precision=lax.Precision.HIGHEST
    ).astype(jnp.bfloat16)
    leading = mapped.shape[:3]
    projected_rows = jnp.dot(
        mapped.reshape(-1, mapped.shape[3]),
        code_raising_operator,
        preferred_element_type=jnp.float32,
    )
    projected_rows = projected_rows.reshape(leading + (code_raising_operator.shape[1],))
    return (projected_rows + placement_tier_features.astype(jnp.float32)).astype(jnp.bfloat16)


def norm_mod(latent_stream, scale_term, offset_term):
    widened = latent_stream.astype(jnp.float32)
    average = jnp.mean(widened, axis=-1, keepdims=True)
    centred = widened - average
    spread = jnp.mean(centred * centred, axis=-1, keepdims=True)
    normed = (
        centred * lax.rsqrt(spread + 1e-06) * (1.0 + scale_term[:, None, :])
        + offset_term[:, None, :]
    )
    return normed.astype(jnp.bfloat16)


def attention(qkv_cols, log_scale, cached_keys, cached_values):
    qkv = lax.all_to_all(qkv_cols, "tp", split_axis=0, concat_axis=3, tiled=True)
    images = qkv.shape[0]
    count = qkv.shape[1]
    widened = qkv.astype(jnp.float32)
    query = widened[:, :, 0].reshape(images, count, FOCUS_GROUPS, HEAD_DIM)
    new_keys = widened[:, :, 1].reshape(images, count, FOCUS_GROUPS, HEAD_DIM)
    new_values = qkv[:, :, 2].reshape(images, count, FOCUS_GROUPS, HEAD_DIM)
    head_mult = jnp.exp(jnp.minimum(log_scale, LOG_CAP))
    query = (
        query
        * lax.rsqrt(jnp.sum(query * query, axis=-1, keepdims=True) + 1e-06)
        * head_mult[:, None]
    )
    new_keys = new_keys * lax.rsqrt(jnp.sum(new_keys * new_keys, axis=-1, keepdims=True) + 1e-06)
    all_keys = jnp.concatenate(
        [cached_keys.astype(jnp.float32).reshape(images, -1, FOCUS_GROUPS, HEAD_DIM), new_keys],
        axis=1,
    )
    all_values = jnp.concatenate(
        [cached_values.reshape(images, -1, FOCUS_GROUPS, HEAD_DIM), new_values], axis=1
    )
    scores = jnp.einsum("iqhd,ikhd->ihqk", query, all_keys, precision=lax.Precision.HIGHEST)
    maximum = jnp.max(scores, axis=-1, keepdims=True)
    weights = jnp.exp(scores - maximum)
    probabilities = (weights / jnp.sum(weights, axis=-1, keepdims=True)).astype(jnp.bfloat16)
    mixed = jnp.einsum(
        "ihqk,ikhd->iqhd", probabilities, all_values, preferred_element_type=jnp.float32
    )
    return mixed.reshape(images, count, FOCUS_GROUPS * HEAD_DIM).astype(jnp.bfloat16)


def project_out(attended, out_matrix):
    return jnp.dot(
        lax.all_gather(attended, "tp", axis=0, tiled=True),
        out_matrix,
        preferred_element_type=jnp.float32,
    )


def pass_on(latent_stream):
    return shifted(latent_stream, "section", 1)


def local(
    awaiting_arrivals,
    label_numbers,
    drawn_coarse_codes,
    discrete_prototypes,
    code_raising_operator,
    placement_tier_features,
    label_feature_rows,
    conditioned_gain_mapping,
    conditioned_shift_addend,
    question_answer_operator,
    mixing_return_operator,
    focus_sharpness_exponents,
    prior_resolution_probes,
    prior_resolution_answers,
):
    sections = lax.axis_size("section")
    section_at = lax.axis_index("section")
    group_index = lax.axis_index("tp")
    moments = prior_resolution_probes.shape[1]
    width = question_answer_operator.shape[1]
    column_width = question_answer_operator.shape[3]
    images = drawn_coarse_codes.shape[1]
    resident_pictures = awaiting_arrivals.shape[1]
    class_rows = lax.dynamic_slice_in_dim(label_numbers, sections - 1 - section_at, moments, 0)
    class_part = jnp.take(label_feature_rows, class_rows, axis=0)
    activated_part = jax.nn.silu(class_part.astype(jnp.float32)).astype(jnp.bfloat16)
    gated_response = lax.all_gather(activated_part, "tp", axis=2, tiled=True)
    flat_active = gated_response.reshape(moments * images, width)
    inner_block = 0
    local_mod = conditioned_gain_mapping[inner_block].reshape(width, 3 * column_width)
    modulated = jnp.dot(flat_active, local_mod, preferred_element_type=jnp.float32)
    mod_list = [
        modulated.reshape(moments, images, 3, column_width) + conditioned_shift_addend[inner_block]
    ]
    mod_cols = jnp.stack(mod_list)
    resample_table = resampler()
    emitted = []
    mod_rows = lax.all_to_all(mod_cols, "tp", split_axis=2, concat_axis=4, tiled=True)
    own_tokens = lax.dynamic_slice_in_dim(
        drawn_coarse_codes, group_index * resident_pictures, resident_pictures, 1
    )
    entering = embed(
        own_tokens,
        discrete_prototypes,
        code_raising_operator,
        placement_tier_features,
        resample_table,
    )
    passed_along_activation = awaiting_arrivals[0]
    for clock_tick in range(moments):
        latent_stream = passed_along_activation
        inner_block = 0
        modulation = mod_rows[inner_block, clock_tick]
        normed = norm_mod(latent_stream, modulation[:, 1], modulation[:, 2])
        local_qkv = question_answer_operator[inner_block].reshape(width, 3 * column_width)

        def body_product(portion, offset, local_qkv=local_qkv):
            return jnp.dot(portion, local_qkv, preferred_element_type=jnp.float32).astype(
                jnp.bfloat16
            )

        qkv_cols = body_product(lax.all_gather(normed, "tp", axis=0, tiled=True), jnp.int32(0))
        qkv_cols = qkv_cols.reshape(qkv_cols.shape[0], qkv_cols.shape[1], 3, column_width)
        attended = attention(
            qkv_cols,
            focus_sharpness_exponents[inner_block],
            prior_resolution_probes[inner_block, clock_tick],
            prior_resolution_answers[inner_block, clock_tick],
        )
        projected_cols = project_out(attended, mixing_return_operator[inner_block]).astype(
            jnp.bfloat16
        )
        projected = lax.all_to_all(projected_cols, "tp", split_axis=0, concat_axis=2, tiled=True)
        latent_stream = (
            latent_stream.astype(jnp.float32)
            + modulation[:, 0][:, None, :] * projected.astype(jnp.float32)
        ).astype(jnp.bfloat16)
        emitted.append(latent_stream)
        if clock_tick + 1 < moments:
            arrived = pass_on(latent_stream)
            passed_along_activation = jnp.where(section_at == 0, entering[clock_tick], arrived)
    result = jnp.stack(emitted)
    return result[None]


def solution(mesh):
    in_specs = (
        P("section", "tp", None, None),
        P(),
        P(),
        P(),
        P(),
        P(),
        P(None, "tp"),
        P("section", None, None, "tp"),
        P("section", None, "tp"),
        P("section", None, None, "tp"),
        P("section", None, "tp"),
        P("section", None),
        P("section", None, "tp", None, None),
        P("section", None, "tp", None, None),
    )
    out_specs = P("section", None, "tp", None, None)
    return jax.shard_map(local, mesh=mesh, in_specs=in_specs, out_specs=out_specs, check_vma=False)
```

profile of v0, /device:TPU:4, one launch (start us, length us, event | category | flops | bytes accessed | tf_op | source)
XLA Modules:
  0.0 244.2 jit_solution(13599707762112273153)
XLA Ops:
  0.9 1.2 copy.162
  3.0 16.4 %all_gather.15 = bf16[2,8,1920]{1,0,2:T(2,128)(2,1)S(1)} all-gather(bf16[2,8,240]{1,0,2:T(2,128)(2,1)S(1)} %copy.163), channel_id=1, replica_groups=mesh['section'=4,'tp'=8] {'tp'}, dimensions={2}, use_global_device_ids=true | all-gather | bytes 69120 | tf_op jit(solution)/shard_map/all_gather | solution.py:144
  20.1 2.9 %fusion.17 = f32[1,2,8,3,240]{4,2,3,1,0:T(8,128)S(1)} fusion(bf16[1,1920,3,240]{1,3,2,0:T(8,128)(2,1)} %param.21, bf16[2,8,1920,1]{1,0,2,3:T(2,128)(2,1)S(1)} %bitcast.178, f32[3,240]{1,0:T(4,128)S(1)} %bitcast.180), kind=kOutput, calls=%fused_computation.24 | convolution fusion | flops 44248320 | bytes 2875200 | tf_op jit(solution)/shard_map/dot_general | solution.py:148
  23.7 5.1 %all-to-all-start = ((f32[1,2,8,3,240]{4,1,3,0,2:T(2,128)}), f32[1,2,8,3,240]{4,1,3,0,2:T(2,128)S(1)}, u32[]{:S(2)}, u32[]{:S(2)}) async-start(f32[1,2,8,3,240]{4,1,3,0,2:T(2,128)} %copy.165), calls=%async_computation | async-start | bytes 98304 | tf_op jit(solution)/shard_map/all_to_all | solution.py:155
  29.2 1.5 convert_reduce_fusion.1
  32.4 2.8 %slice_reduce_fusion = (bf16[30,1920]{1,0:T(8,128)(2,1)}, bf16[30,1920]{1,0:T(8,128)(2,1)}) fusion(bf16[1,2,1,30,1920]{4,1,3,2,0:T(2,128)(2,1)} %param.27), kind=kLoop, calls=%fused_computation.77 | loop fusion | bytes 460800 | tf_op jit(solution)/shard_map/slice | solution.py:185
  36.7 17.0 %all_gather.16 = bf16[8,25,1920]{2,1,0:T(8,128)(2,1)S(1)} all-gather(bf16[1,25,1920]{2,1,0:T(8,128)(2,1)S(1)} %fusion.43), channel_id=1, replica_groups=mesh['section'=4,'tp'=8] {'tp'}, dimensions={0}, use_global_device_ids=true | all-gather | bytes 864000 | tf_op jit(solution)/shard_map/all_gather | solution.py:179
  53.6 1.8 convolution_convert_fusion.1
  55.4 1.7 reshape.1148
  58.0 5.2 %all-to-all-start.1 = ((bf16[8,25,3,240]{3,1,2,0:T(8,128)(2,1)}), bf16[8,25,3,240]{3,1,2,0:T(8,128)(2,1)}, u32[]{:S(2)}, u32[]{:S(2)}) async-start(bf16[8,25,3,240]{3,1,2,0:T(8,128)(2,1)} %copy.169), calls=%async_computation.1 | async-start | bytes 786432 | tf_op jit(solution)/shard_map/all_to_all | solution.py:74
  67.0 3.0 %copy.180 = f32[4096,32]{1,0:T(8,128)} copy(f32[4096,32]{0,1:T(8,128)} %param.17) | data formatting | bytes 1048576 | tf_op args[3]
  73.9 2.8 %gather_fusion.1 = f32[30,32]{1,0:T(8,128)} fusion(f32[4096,32]{1,0:T(8,128)} %copy.180, s32[1024]{0:T(1024)S(1)} %pad_clamp_fusion), kind=kCustom, calls=%fused_computation.1 | custom fusion | bytes 7800 | tf_op jit(solution)/shard_map/gather | solution.py:47
  82.2 1.4 copy.173
  83.6 1.8 copy_multiply_fusion.1
  86.5 1.7 slice_multiply_fusion.1
  88.1 1.9 mul.390
  91.4 2.8 %fusion.24 = f32[30,25,55]{2,1,0:T(8,128)S(1)} fusion(f32[1,25,30,64]{3,1,2,0:T(8,128)} %copy_multiply_fusion.1, f32[1,30,30,64]{3,1,2,0:T(8,128)} %copy.175, f32[25,30,64]{2,1,0:T(8,128)S(1)} %multiply_multiply_fusion.1), kind=kOutput, calls=%fused_computation.31 | convolution fusion | flops 31785600 | bytes 779400 | tf_op jit(solution)/shard_map/iqhd,ikhd->ihqk/dot_general | solution.py:95
  95.5 1.7 copy.172
  97.2 3.5 %fusion.12 = bf16[1,25,30,64]{3,1,2,0:T(8,128)(2,1)} fusion(bf16[1,25,30,64]{3,1,2,0:T(8,128)(2,1)} %copy.172, bf16[1,30,30,64]{3,1,2,0:T(8,128)(2,1)} %copy.171, f32[30,25]{1,0:T(8,128)S(1)} %fusion.73, f32[30,25,55]{2,1,0:T(8,128)S(1)} %fusion.24), kind=kOutput, calls=%fused_computation.19 | convolution fusion | flops 5874954 | bytes 475200 | tf_op jit(solution)/shard_map/ihqk,ikhd->iqhd/dot_general | solution.py:99
  102.0 17.0 %all_gather.17 = bf16[8,25,1920]{2,1,0:T(8,128)(2,1)S(1)} all-gather(bf16[1,25,1920]{2,1,0:T(8,128)(2,1)S(1)} %convert_element_type.264), channel_id=1, replica_groups=mesh['section'=4,'tp'=8] {'tp'}, dimensions={0}, use_global_device_ids=true | all-gather | bytes 864000 | tf_op jit(solution)/shard_map/all_gather | solution.py:107
  119.0 2.3 convolution_convert_fusion.5
  121.2 5.2 %all-to-all-start.2 = ((bf16[8,25,240]{2,1,0:T(8,128)(2,1)}), bf16[8,25,240]{2,1,0:T(8,128)(2,1)S(1)}, u32[]{:S(2)}, u32[]{:S(2)}) async-start(bf16[8,25,240]{2,1,0:T(8,128)(2,1)} %convolution_convert_fusion.5), calls=%async_computation.2 | async-start | bytes 262144 | tf_op jit(solution)/shard_map/all_to_all | solution.py:190
  126.7 6.5 %all-to-all-done.2 = bf16[8,25,240]{2,1,0:T(8,128)(2,1)S(1)} async-done(((bf16[8,25,240]{2,1,0:T(8,128)(2,1)}), bf16[8,25,240]{2,1,0:T(8,128)(2,1)S(1)}, u32[]{:S(2)}, u32[]{:S(2)}) %all-to-all-start.2) | async-done | bytes 96032 | tf_op jit(solution)/shard_map/all_to_all | solution.py:190
  133.6 3.4 %collective-permute-start = (bf16[1,25,1920]{2,1,0:T(8,128)(2,1)S(1)}, bf16[1,25,1920]{2,1,0:T(8,128)(2,1)S(1)}, u32[]{:S(2)}, u32[]{:S(2)}) collective-permute-start(bf16[1,25,1920]{2,1,0:T(8,128)(2,1)S(1)} %fusion.44), channel_id=1, source_target_pairs={{0,8},{8,16},{16,24},{1,9},{9,17},{17,25},{2,10},{10,18},{18,26},{... | collective-permute-start | bytes 288008 | tf_op jit(solution)/shard_map/ppermute | solution.py:15
  137.6 3.6 %collective-permute-done = bf16[1,25,1920]{2,1,0:T(8,128)(2,1)S(1)} collective-permute-done((bf16[1,25,1920]{2,1,0:T(8,128)(2,1)S(1)}, bf16[1,25,1920]{2,1,0:T(8,128)(2,1)S(1)}, u32[]{:S(2)}, u32[]{:S(2)}) %collective-permute-start) | collective-permute-done | bytes 96032 | tf_op jit(solution)/shard_map/ppermute | solution.py:15
  141.2 1.3 fusion.74
  142.9 16.3 %all_gather.18 = bf16[8,25,1920]{2,1,0:T(8,128)(2,1)S(1)} all-gather(bf16[1,25,1920]{2,1,0:T(8,128)(2,1)S(1)} %add_convert_fusion.1), channel_id=1, replica_groups=mesh['section'=4,'tp'=8] {'tp'}, dimensions={0}, use_global_device_ids=true | all-gather | bytes 864000 | tf_op jit(solution)/shard_map/all_gather | solution.py:179
  159.2 1.8 convolution_convert_fusion
  161.0 2.4 reshape.1151
  163.4 1.8 copy.187
  165.2 4.3 %all-to-all-start.3 = ((bf16[8,25,3,240]{3,1,2,0:T(8,128)(2,1)}), bf16[8,25,3,240]{3,1,2,0:T(8,128)(2,1)}, u32[]{:S(2)}, u32[]{:S(2)}) async-start(bf16[8,25,3,240]{3,1,2,0:T(8,128)(2,1)} %copy.187), calls=%async_computation.3 | async-start | bytes 786432 | tf_op jit(solution)/shard_map/all_to_all | solution.py:74
  169.5 2.0 reshape.1119
  171.5 2.1 copy.193
  174.5 1.7 copy.189
  177.1 4.7 %all-to-all-done.3 = bf16[8,25,3,240]{3,1,2,0:T(8,128)(2,1)} async-done(((bf16[8,25,3,240]{3,1,2,0:T(8,128)(2,1)}), bf16[8,25,3,240]{3,1,2,0:T(8,128)(2,1)}, u32[]{:S(2)}, u32[]{:S(2)}) %all-to-all-start.3) | async-done | bytes 288032 | tf_op jit(solution)/shard_map/all_to_all | solution.py:74
  181.8 1.9 copy.188
  183.7 1.4 all_to_all.65
  186.8 1.9 mul.431
  189.9 1.9 reshape_squeeze.39
  191.8 1.9 reshape_squeeze.40
  196.4 1.3 copy_multiply_fusion
  198.8 2.7 %fusion.27 = f32[30,25,55]{2,1,0:T(8,128)S(1)} fusion(f32[1,25,30,64]{3,1,2,0:T(8,128)S(1)} %copy_multiply_fusion, f32[1,30,30,64]{3,1,2,0:T(8,128)} %copy.193, f32[25,30,64]{2,1,0:T(8,128)S(1)} %multiply_multiply_fusion), kind=kOutput, calls=%fused_computation.35 | convolution fusion | flops 31785600 | bytes 779400 | tf_op jit(solution)/shard_map/iqhd,ikhd->ihqk/dot_general | solution.py:95
  203.6 3.8 %fusion.13 = bf16[1,25,30,64]{3,1,2,0:T(8,128)(2,1)} fusion(bf16[1,25,30,64]{3,1,2,0:T(8,128)(2,1)} %copy.190, bf16[1,30,30,64]{3,1,2,0:T(8,128)(2,1)} %copy.189, f32[30,25]{1,0:T(8,128)S(1)} %fusion.75, f32[30,25,55]{2,1,0:T(8,128)} %copy-done.5), kind=kOutput, calls=%fused_computation.20 | convolution fusion | flops 5874954 | bytes 475200 | tf_op jit(solution)/shard_map/ihqk,ikhd->iqhd/dot_general | solution.py:99
  207.4 1.7 copy.195
  210.3 16.2 %all_gather.19 = bf16[8,25,1920]{2,1,0:T(8,128)(2,1)S(1)} all-gather(bf16[1,25,1920]{2,1,0:T(8,128)(2,1)S(1)} %convert_element_type.289), channel_id=1, replica_groups=mesh['section'=4,'tp'=8] {'tp'}, dimensions={0}, use_global_device_ids=true | all-gather | bytes 864000 | tf_op jit(solution)/shard_map/all_gather | solution.py:107
  226.5 2.3 convolution_convert_fusion.4
  228.8 4.0 %all-to-all-start.4 = ((bf16[8,25,240]{2,1,0:T(8,128)(2,1)}), bf16[8,25,240]{2,1,0:T(8,128)(2,1)}, u32[]{:S(2)}, u32[]{:S(2)}) async-start(bf16[8,25,240]{2,1,0:T(8,128)(2,1)} %convolution_convert_fusion.4), calls=%async_computation.4 | async-start | bytes 262144 | tf_op jit(solution)/shard_map/all_to_all | solution.py:190
  233.5 6.1 %all-to-all-done.4 = bf16[8,25,240]{2,1,0:T(8,128)(2,1)} async-done(((bf16[8,25,240]{2,1,0:T(8,128)(2,1)}), bf16[8,25,240]{2,1,0:T(8,128)(2,1)}, u32[]{:S(2)}, u32[]{:S(2)}) %all-to-all-start.4) | async-done | bytes 96032 | tf_op jit(solution)/shard_map/all_to_all | solution.py:190
  (142 shorter events, 44.2 us)
Async XLA Ops:
  0.0 53.6 %copy-start = (bf16[1,1920,3,240]{1,3,2,0:T(8,128)(2,1)S(1)}, bf16[1,1920,3,240]{1,3,2,0:T(8,128)(2,1)}, u32[]{:S(2)}) copy-start(bf16[1,1920,3,240]{1,3,2,0:T(8,128)(2,1)} %param.23) | copy-start | bytes 8294404
  2.2 26.7 %copy-start.3 = (bf16[1,1,25,1920]{3,2,1,0:T(8,128)(2,1)S(1)}, bf16[1,1,25,1920]{3,2,1,0:T(8,128)(2,1)}, u32[]{:S(2)}) copy-start(bf16[1,1,25,1920]{3,2,1,0:T(8,128)(2,1)} %param.14) | copy-start | bytes 288004
  2.8 26.5 %copy-start.7 = (bf16[1,2,1,30,1920]{4,1,3,2,0:T(2,128)(2,1)S(1)}, bf16[1,2,1,30,1920]{4,1,3,2,0:T(2,128)(2,1)}, u32[]{:S(2)}) copy-start(bf16[1,2,1,30,1920]{4,1,3,2,0:T(2,128)(2,1)} %param.26) | copy-start | bytes 691204
  23.7 11.5 %all-to-all-start = ((f32[1,2,8,3,240]{4,1,3,0,2:T(2,128)}), f32[1,2,8,3,240]{4,1,3,0,2:T(2,128)S(1)}, u32[]{:S(2)}, u32[]{:S(2)}) async-start(f32[1,2,8,3,240]{4,1,3,0,2:T(2,128)} %copy.165), calls=%async_computation | async-start | bytes 98304 | tf_op jit(solution)/shard_map/all_to_all | solution.py:155
  58.0 18.7 %all-to-all-start.1 = ((bf16[8,25,3,240]{3,1,2,0:T(8,128)(2,1)}), bf16[8,25,3,240]{3,1,2,0:T(8,128)(2,1)}, u32[]{:S(2)}, u32[]{:S(2)}) async-start(bf16[8,25,3,240]{3,1,2,0:T(8,128)(2,1)} %copy.169), calls=%async_computation.1 | async-start | bytes 786432 | tf_op jit(solution)/shard_map/all_to_all | solution.py:74
  64.0 6.7 %copy-start.9 = (f32[5,5,3,3]{1,0,3,2:T(8,128)S(1)}, f32[5,5,3,3]{1,0,3,2:T(8,128)}, u32[]{:S(2)}) copy-start(f32[5,5,3,3]{1,0,3,2:T(8,128)} %broadcast_multiply_fusion.1) | copy-start | bytes 2704
  64.0 7.5 %copy-start.12 = (f32[5,5,2,2]{1,0,3,2:T(8,128)S(1)}, f32[5,5,2,2]{1,0,3,2:T(8,128)}, u32[]{:S(2)}) copy-start(f32[5,5,2,2]{1,0,3,2:T(8,128)} %broadcast_multiply_fusion.2) | copy-start | bytes 1204
  64.0 8.3 %copy-start.19 = (f32[5]{0:T(128)S(1)}, f32[5]{0:T(128)}, u32[]{:S(2)}) copy-start(f32[5]{0:T(128)} %maximum_multiply_fusion.3) | copy-start | bytes 64
  64.0 12.7 %copy-start.20 = (f32[1,30]{1,0:T(1,128)S(1)}, f32[1,30]{1,0:T(1,128)}, u32[]{:S(2)}) copy-start(f32[1,30]{1,0:T(1,128)} %param.25) | copy-start | bytes 364
  78.4 9.8 %copy-start.1 = (bf16[1,25,3,1920]{3,1,2,0:T(8,128)(2,1)}, bf16[1,25,3,1920]{3,1,2,0:T(8,128)(2,1)S(1)}, u32[]{:S(2)}) copy-start(bf16[1,25,3,1920]{3,1,2,0:T(8,128)(2,1)S(1)} %all_to_all.60) | copy-start | bytes 864004
  90.0 4.6 %slice-start = ((bf16[1,25,3,1920]{3,1,2,0:T(8,128)(2,1)}), bf16[1,25,1,1920]{3,1,2,0:T(8,128)(2,1)S(1)}, s32[]{:S(2)}) async-start(bf16[1,25,3,1920]{3,1,2,0:T(8,128)(2,1)} %copy-done.1), calls=%async_computation.5 | async-start | bytes 245760 | tf_op jit(solution)/shard_map/slice | solution.py:80
  100.6 25.8 %copy-start.13 = (f32[30,32]{1,0:T(8,128)S(1)}, f32[30,32]{1,0:T(8,128)}, u32[]{:S(2)}) copy-start(f32[30,32]{1,0:T(8,128)} %gather_fusion.1) | copy-start | bytes 11524
  100.6 25.8 %copy-start.14 = (f32[25,9]{1,0:T(8,128)S(1)}, f32[25,9]{1,0:T(8,128)}, u32[]{:S(2)}) copy-start(f32[25,9]{1,0:T(8,128)} %copy.183) | copy-start | bytes 2704
  100.6 25.8 %copy-start.15 = (f32[25,4]{1,0:T(8,128)S(1)}, f32[25,4]{1,0:T(8,128)}, u32[]{:S(2)}) copy-start(f32[25,4]{1,0:T(8,128)} %copy.182) | copy-start | bytes 1204
  100.6 25.8 %copy-start.16 = (f32[25,1]{1,0:T(8,128)S(1)}, f32[25,1]{1,0:T(8,128)}, u32[]{:S(2)}) copy-start(f32[25,1]{1,0:T(8,128)} %copy.181) | copy-start | bytes 304
  100.6 25.8 %copy-start.17 = (f32[25,16]{1,0:T(8,128)S(1)}, f32[25,16]{1,0:T(8,128)}, u32[]{:S(2)}) copy-start(f32[25,16]{1,0:T(8,128)} %mul.419) | copy-start | bytes 4804
  100.7 32.9 %copy-start.4 = (bf16[1,1,25,1920]{3,2,1,0:T(8,128)(2,1)S(1)}, bf16[1,1,25,1920]{3,2,1,0:T(8,128)(2,1)}, u32[]{:S(2)}) copy-start(bf16[1,1,25,1920]{3,2,1,0:T(8,128)(2,1)} %param.14) | copy-start | bytes 288004
  100.7 32.9 %copy-start.11 = (f32[1920]{0:T(1024)S(1)}, f32[1920]{0:T(1024)}, u32[]{:S(2)}) copy-start(f32[1920]{0:T(1024)} %get-tuple-element.12) | copy-start | bytes 23044
  101.8 35.2 %copy-start.10 = (f32[1,3,1920]{2,0,1:T(1,128)S(1)}, f32[1,3,1920]{2,0,1:T(1,128)}, u32[]{:S(2)}) copy-start(f32[1,3,1920]{2,0,1:T(1,128)} %get-tuple-element.21) | copy-start | bytes 69124
  121.2 11.9 %all-to-all-start.2 = ((bf16[8,25,240]{2,1,0:T(8,128)(2,1)}), bf16[8,25,240]{2,1,0:T(8,128)(2,1)S(1)}, u32[]{:S(2)}, u32[]{:S(2)}) async-start(bf16[8,25,240]{2,1,0:T(8,128)(2,1)} %convolution_convert_fusion.5), calls=%async_computation.2 | async-start | bytes 262144 | tf_op jit(solution)/shard_map/all_to_all | solution.py:190
  133.6 7.7 %collective-permute-start = (bf16[1,25,1920]{2,1,0:T(8,128)(2,1)S(1)}, bf16[1,25,1920]{2,1,0:T(8,128)(2,1)S(1)}, u32[]{:S(2)}, u32[]{:S(2)}) collective-permute-start(bf16[1,25,1920]{2,1,0:T(8,128)(2,1)S(1)} %fusion.44), channel_id=1, source_target_pairs={{0,8},{8,16},{16,24},{1,9},{9,17},{17,25},{2,10},{10,18},{18,26},{... | collective-permute-start | bytes 288008 | tf_op jit(solution)/shard_map/ppermute | solution.py:15
  161.0 12.6 %copy-start.8 = (bf16[30,1920]{1,0:T(8,128)(2,1)S(1)}, bf16[30,1920]{1,0:T(8,128)(2,1)}, u32[]{:S(2)}) copy-start(bf16[30,1920]{1,0:T(8,128)(2,1)} %get-tuple-element.7) | copy-start | bytes 345604
  165.2 16.6 %all-to-all-start.3 = ((bf16[8,25,3,240]{3,1,2,0:T(8,128)(2,1)}), bf16[8,25,3,240]{3,1,2,0:T(8,128)(2,1)}, u32[]{:S(2)}, u32[]{:S(2)}) async-start(bf16[8,25,3,240]{3,1,2,0:T(8,128)(2,1)} %copy.187), calls=%async_computation.3 | async-start | bytes 786432 | tf_op jit(solution)/shard_map/all_to_all | solution.py:74
  185.2 9.7 %copy-start.2 = (bf16[1,25,3,1920]{3,1,2,0:T(8,128)(2,1)}, bf16[1,25,3,1920]{3,1,2,0:T(8,128)(2,1)S(1)}, u32[]{:S(2)}) copy-start(bf16[1,25,3,1920]{3,1,2,0:T(8,128)(2,1)S(1)} %all_to_all.65) | copy-start | bytes 864004
  195.5 7.1 %slice-start.1 = ((bf16[1,25,3,1920]{3,1,2,0:T(8,128)(2,1)}), bf16[1,25,1,1920]{3,1,2,0:T(8,128)(2,1)S(1)}, s32[]{:S(2)}) async-start(bf16[1,25,3,1920]{3,1,2,0:T(8,128)(2,1)} %copy-done.2), calls=%async_computation.6 | async-start | bytes 245760 | tf_op jit(solution)/shard_map/slice | solution.py:80
  201.5 0.8 copy-start.5
  207.4 25.4 %copy-start.6 = (f32[1,1,25,1920]{3,2,1,0:T(8,128)S(1)}, f32[1,1,25,1920]{3,2,1,0:T(8,128)}, u32[]{:S(2)}) copy-start(f32[1,1,25,1920]{3,2,1,0:T(8,128)} %reshape.1149) | copy-start | bytes 576004
  209.2 33.2 %copy-start.18 = (f32[1920]{0:T(1024)S(1)}, f32[1920]{0:T(1024)}, u32[]{:S(2)}) copy-start(f32[1920]{0:T(1024)} %get-tuple-element.9) | copy-start | bytes 23044
  228.8 10.8 %all-to-all-start.4 = ((bf16[8,25,240]{2,1,0:T(8,128)(2,1)}), bf16[8,25,240]{2,1,0:T(8,128)(2,1)}, u32[]{:S(2)}, u32[]{:S(2)}) async-start(bf16[8,25,240]{2,1,0:T(8,128)(2,1)} %convolution_convert_fusion.4), calls=%async_computation.4 | async-start | bytes 262144 | tf_op jit(solution)/shard_map/all_to_all | solution.py:190
where the time goes:
time: 246 us; the launch traced here: 244 us
  blocking collectives  82.9 us (34%)
  local copies, waits for them, and re-layouts  63.8 us (26%)
  starting transfers between devices  27.2 us (11%)
  matrix products  25.3 us (10%)
  other arithmetic  23.5 us (10%)
  waiting for transfers between devices  20.9 us (8%)
    all_gather x2, blocking collectives, local(): lax.all_gather(normed, 'tp', axis=0, tiled=True)  33.3 us
    all_gather x2, blocking collectives, project_out(): lax.all_gather(attended, 'tp', axis=0, tiled=True)  33.2 us
    all_gather x1, blocking collectives, local(): gated_response = lax.all_gather(activated_part, 'tp', axis=2, tiled=True)  16.4 us
    all_to_all x2, waiting for transfers between devices, local(): lax.all_to_all(projected_cols, 'tp', split_axis=0, concat_axis=2, tiled=T...  12.5 us
    all_to_all x2, starting transfers between devices, attention(): lax.all_to_all(qkv_cols, 'tp', split_axis=0, concat_axis=3, tiled=True)  9.52 us
    all_to_all x2, starting transfers between devices, local(): lax.all_to_all(projected_cols, 'tp', split_axis=0, concat_axis=2, tiled=T...  9.2 us
    dot_general x2, matrix products, attention(): jnp.einsum('ihqk,ikhd->iqhd', probabilities, all_values, preferred_elemen...  7.32 us
    reshape x4, local copies, waits for them, and re-layouts, local(): qkv_cols.reshape(qkv_cols.shape[0], qkv_cols.shape[1], 3, column_width)  6.8 us
  transfers between devices with their start and end apart: 6, of which 4 were waited for; matrix products, arithmetic and copies ran while one was open for 12% of the time, Pallas kernels for 0%

commit v1 on v0

--- a/solution.py
+++ b/solution.py
@@ -71,7 +71,10 @@
 
 
 def attention(qkv_cols, log_scale, cached_keys, cached_values):
-    qkv = lax.all_to_all(qkv_cols, "tp", split_axis=0, concat_axis=3, tiled=True)
+    qkv = jnp.concatenate(
+        lax.all_to_all(jnp.stack(jnp.split(qkv_cols, lax.axis_size("tp"), axis=0)), "tp", 0, 0),
+        axis=3,
+    )
     images = qkv.shape[0]
     count = qkv.shape[1]
     widened = qkv.astype(jnp.float32)

time: 246 us -> 268 us (1.089)
  local copies, waits for them, and re-layouts: 63.8 us -> 82 us
  waiting for transfers between devices: 20.9 us -> 26.6 us
    another operation x0 -> x20, local copies, waits for them, and re-layouts: none -> 17.4 us  [attention(): jnp.stack(jnp.split(qkv_cols, lax.axis_size('tp'), axis=0))]
    unnamed x45 -> x63, local copies, waits for them, and re-layouts: 5.77 us -> 14.5 us
    all_to_all x2, waiting for transfers between devices: 4.72 us -> 11.2 us  [attention(): lax.all_to_all(jnp.stack(jnp.split(qkv_cols, lax.axis_size('tp'), axis=0)...]
    all_to_all x4 -> x0, local copies, waits for them, and re-layouts: 4.97 us -> none  [attention(): lax.all_to_all(qkv_cols, 'tp', split_axis=0, concat_axis=3, tiled=True)]
    reshape x4, local copies, waits for them, and re-layouts: 6.8 us -> 3.97 us  [attention(): jnp.concatenate(lax.all_to_all(jnp.stack(jnp.split(qkv_cols, lax.axis_siz...]
  transfers between devices with their start and end apart: 6 -> 6, of which waited for: 4 -> 5; matrix products, arithmetic and copies ran while one was open for 12% -> 11% of each run, Pallas kernels for 0% -> 0%
where the time goes in v1:
time: 268 us; the launch traced here: 265 us
  blocking collectives  82.3 us (31%)
  local copies, waits for them, and re-layouts  82 us (31%)
  waiting for transfers between devices  26.6 us (10%)
  starting transfers between devices  25.4 us (9%)
  matrix products  24.3 us (9%)
  other arithmetic  24 us (9%)
    all_gather x2, blocking collectives, local(): lax.all_gather(normed, 'tp', axis=0, tiled=True)  33.3 us
    all_gather x2, blocking collectives, project_out(): lax.all_gather(attended, 'tp', axis=0, tiled=True)  32.6 us
    another operation x20, local copies, waits for them, and re-layouts, attention(): jnp.stack(jnp.split(qkv_cols, lax.axis_size('tp'), axis=0))  17.4 us
    all_gather x1, blocking collectives, local(): gated_response = lax.all_gather(activated_part, 'tp', axis=2, tiled=True)  16.4 us
    unnamed x63, local copies, waits for them, and re-layouts  14.5 us
    all_to_all x2, waiting for transfers between devices, local(): lax.all_to_all(projected_cols, 'tp', split_axis=0, concat_axis=2, tiled=T...  11.8 us
    all_to_all x2, waiting for transfers between devices, attention(): lax.all_to_all(jnp.stack(jnp.split(qkv_cols, lax.axis_size('tp'), axis=0)...  11.2 us
    all_to_all x2, starting transfers between devices, attention(): lax.all_to_all(jnp.stack(jnp.split(qkv_cols, lax.axis_size('tp'), axis=0)...  9.52 us
  transfers between devices with their start and end apart: 6, of which 5 were waited for; matrix products, arithmetic and copies ran while one was open for 11% of the time, Pallas kernels for 0%

profile of v1, /device:TPU:4, one launch (start us, length us, event | category | flops | bytes accessed | tf_op | source)
XLA Modules:
  0.0 265.4 jit_solution(15038861203110491034)
XLA Ops:
  4.4 16.4 %all_gather.15 = bf16[2,8,1920]{1,0,2:T(2,128)(2,1)S(1)} all-gather(bf16[2,8,240]{1,0,2:T(2,128)(2,1)S(1)} %copy.155), channel_id=1, replica_groups=mesh['section'=4,'tp'=8] {'tp'}, dimensions={2}, use_global_device_ids=true | all-gather | bytes 69120 | tf_op jit(solution)/shard_map/all_gather | solution.py:147
  21.5 2.9 %fusion.17 = f32[1,2,8,3,240]{4,2,3,1,0:T(8,128)S(1)} fusion(bf16[1,1920,3,240]{1,3,2,0:T(8,128)(2,1)} %param.21, bf16[2,8,1920,1]{1,0,2,3:T(2,128)(2,1)S(1)} %bitcast.174, f32[3,240]{1,0:T(4,128)S(1)} %bitcast.176), kind=kOutput, calls=%fused_computation.24 | convolution fusion | flops 44248320 | bytes 2875200 | tf_op jit(solution)/shard_map/dot_general | solution.py:151
  25.1 5.1 %all-to-all-start = ((f32[1,2,8,3,240]{4,1,3,0,2:T(2,128)}), f32[1,2,8,3,240]{4,1,3,0,2:T(2,128)}, u32[]{:S(2)}, u32[]{:S(2)}) async-start(f32[1,2,8,3,240]{4,1,3,0,2:T(2,128)} %copy.157), calls=%async_computation | async-start | bytes 98304 | tf_op jit(solution)/shard_map/all_to_all | solution.py:158
  31.2 1.9 convert_reduce_fusion.1
  34.7 1.6 slice_reduce_fusion
  39.5 3.0 %copy.171 = f32[4096,32]{1,0:T(8,128)} copy(f32[4096,32]{0,1:T(8,128)} %param.17) | data formatting | bytes 1048576 | tf_op args[3]
  46.4 17.0 %all_gather.16 = bf16[8,25,1920]{2,1,0:T(8,128)(2,1)S(1)} all-gather(bf16[1,25,1920]{2,1,0:T(8,128)(2,1)S(1)} %fusion.43), channel_id=1, replica_groups=mesh['section'=4,'tp'=8] {'tp'}, dimensions={0}, use_global_device_ids=true | all-gather | bytes 864000 | tf_op jit(solution)/shard_map/all_gather | solution.py:182
  68.6 5.2 %all-to-all-start.1 = ((bf16[8,1,25,3,240]{4,2,3,1,0:T(8,128)(2,1)}), bf16[8,1,25,3,240]{4,2,3,1,0:T(8,128)(2,1)S(1)}, u32[]{:S(2)}, u32[]{:S(2)}) async-start(bf16[8,1,25,3,240]{4,2,3,1,0:T(8,128)(2,1)} %copy.160), calls=%async_computation.1 | async-start | bytes 786432 | tf_op jit(solution)/shard_map/all_to_all | solution.py:75
  76.4 2.9 %gather_fusion.1 = f32[30,32]{1,0:T(8,128)} fusion(f32[4096,32]{1,0:T(8,128)} %copy.171, s32[1024]{0:T(1024)} %get-tuple-element.41), kind=kCustom, calls=%fused_computation.1 | custom fusion | bytes 7800 | tf_op jit(solution)/shard_map/gather | solution.py:47
  79.9 6.4 %all-to-all-done.1 = bf16[8,1,25,3,240]{4,2,3,1,0:T(8,128)(2,1)S(1)} async-done(((bf16[8,1,25,3,240]{4,2,3,1,0:T(8,128)(2,1)}), bf16[8,1,25,3,240]{4,2,3,1,0:T(8,128)(2,1)S(1)}, u32[]{:S(2)}, u32[]{:S(2)}) %all-to-all-start.1) | async-done | bytes 288032 | tf_op jit(solution)/shard_map/all_to_all | solution.py:75
  91.9 1.9 reshape_squeeze.35
  98.1 2.7 %fusion.24 = f32[30,25,55]{2,1,0:T(8,128)S(1)} fusion(f32[1,25,30,64]{3,1,2,0:T(8,128)S(1)} %copy_multiply_fusion.1, f32[1,30,30,64]{3,1,2,0:T(8,128)} %copy.166, f32[25,30,64]{2,1,0:T(8,128)S(1)} %multiply_multiply_fusion.1), kind=kOutput, calls=%fused_computation.31 | convolution fusion | flops 31785600 | bytes 779400 | tf_op jit(solution)/shard_map/iqhd,ikhd->ihqk/dot_general | solution.py:98
  102.0 1.7 copy.163
  103.7 3.5 %fusion.12 = bf16[1,25,30,64]{3,1,2,0:T(8,128)(2,1)} fusion(bf16[1,25,30,64]{3,1,2,0:T(8,128)(2,1)} %copy.163, bf16[1,30,30,64]{3,1,2,0:T(8,128)(2,1)} %copy.162, f32[30,25]{1,0:T(8,128)S(1)} %fusion.75, f32[30,25,55]{2,1,0:T(8,128)S(1)} %fusion.24), kind=kOutput, calls=%fused_computation.19 | convolution fusion | flops 5874954 | bytes 475200 | tf_op jit(solution)/shard_map/ihqk,ikhd->iqhd/dot_general | solution.py:102
  108.5 16.4 %all_gather.17 = bf16[8,25,1920]{2,1,0:T(8,128)(2,1)S(1)} all-gather(bf16[1,25,1920]{2,1,0:T(8,128)(2,1)S(1)} %convert_element_type.264), channel_id=1, replica_groups=mesh['section'=4,'tp'=8] {'tp'}, dimensions={0}, use_global_device_ids=true | all-gather | bytes 864000 | tf_op jit(solution)/shard_map/all_gather | solution.py:110
  124.8 2.3 convolution_convert_fusion.5
  127.1 3.4 %all-to-all-start.2 = ((bf16[8,25,240]{2,1,0:T(8,128)(2,1)}), bf16[8,25,240]{2,1,0:T(8,128)(2,1)S(1)}, u32[]{:S(2)}, u32[]{:S(2)}) async-start(bf16[8,25,240]{2,1,0:T(8,128)(2,1)} %convolution_convert_fusion.5), calls=%async_computation.2 | async-start | bytes 262144 | tf_op jit(solution)/shard_map/all_to_all | solution.py:193
  131.4 5.8 %all-to-all-done.2 = bf16[8,25,240]{2,1,0:T(8,128)(2,1)S(1)} async-done(((bf16[8,25,240]{2,1,0:T(8,128)(2,1)}), bf16[8,25,240]{2,1,0:T(8,128)(2,1)S(1)}, u32[]{:S(2)}, u32[]{:S(2)}) %all-to-all-start.2) | async-done | bytes 96032 | tf_op jit(solution)/shard_map/all_to_all | solution.py:193
  137.6 3.4 %collective-permute-start = (bf16[1,25,1920]{2,1,0:T(8,128)(2,1)S(1)}, bf16[1,25,1920]{2,1,0:T(8,128)(2,1)S(1)}, u32[]{:S(2)}, u32[]{:S(2)}) collective-permute-start(bf16[1,25,1920]{2,1,0:T(8,128)(2,1)S(1)} %fusion.44), channel_id=1, source_target_pairs={{0,8},{8,16},{16,24},{1,9},{9,17},{17,25},{2,10},{10,18},{18,26},{... | collective-permute-start | bytes 288008 | tf_op jit(solution)/shard_map/ppermute | solution.py:15
  141.6 3.6 %collective-permute-done = bf16[1,25,1920]{2,1,0:T(8,128)(2,1)S(1)} collective-permute-done((bf16[1,25,1920]{2,1,0:T(8,128)(2,1)S(1)}, bf16[1,25,1920]{2,1,0:T(8,128)(2,1)S(1)}, u32[]{:S(2)}, u32[]{:S(2)}) %collective-permute-start) | collective-permute-done | bytes 96032 | tf_op jit(solution)/shard_map/ppermute | solution.py:15
  146.9 16.3 %all_gather.18 = bf16[8,25,1920]{2,1,0:T(8,128)(2,1)S(1)} all-gather(bf16[1,25,1920]{2,1,0:T(8,128)(2,1)S(1)} %add_convert_fusion.1), channel_id=1, replica_groups=mesh['section'=4,'tp'=8] {'tp'}, dimensions={0}, use_global_device_ids=true | all-gather | bytes 864000 | tf_op jit(solution)/shard_map/all_gather | solution.py:182
  166.6 1.5 stack.75
  168.1 1.5 stack.76
  169.6 1.5 stack.77
  171.2 1.5 stack.78
  172.7 1.5 stack.79
  175.1 1.5 stack.81
  176.6 1.4 constant_dynamic-update-slice_fusion.14
  178.1 1.4 constant_dynamic-update-slice_fusion.13
  180.9 1.4 constant_dynamic-update-slice_fusion.11
  182.4 1.4 constant_dynamic-update-slice_fusion.10
  185.9 1.8 copy.177
  187.7 4.3 %all-to-all-start.3 = ((bf16[8,1,25,3,240]{4,2,3,1,0:T(8,128)(2,1)}), bf16[8,1,25,3,240]{4,2,3,1,0:T(8,128)(2,1)}, u32[]{:S(2)}, u32[]{:S(2)}) async-start(bf16[8,1,25,3,240]{4,2,3,1,0:T(8,128)(2,1)} %copy.177), calls=%async_computation.3 | async-start | bytes 786432 | tf_op jit(solution)/shard_map/all_to_all | solution.py:75
  192.0 2.0 reshape.1161
  194.0 2.1 copy.183
  197.0 1.7 copy.179
  199.6 4.7 %all-to-all-done.3 = bf16[8,1,25,3,240]{4,2,3,1,0:T(8,128)(2,1)} async-done(((bf16[8,1,25,3,240]{4,2,3,1,0:T(8,128)(2,1)}), bf16[8,1,25,3,240]{4,2,3,1,0:T(8,128)(2,1)}, u32[]{:S(2)}, u32[]{:S(2)}) %all-to-all-start.3) | async-done | bytes 288032 | tf_op jit(solution)/shard_map/all_to_all | solution.py:75
  204.4 1.9 copy.178
  209.3 1.9 mul.431
  212.4 1.9 reshape_squeeze.39
  214.3 1.9 reshape_squeeze.40
  220.0 2.7 %fusion.27 = f32[30,25,55]{2,1,0:T(8,128)S(1)} fusion(f32[1,25,30,64]{3,1,2,0:T(8,128)S(1)} %copy_multiply_fusion, f32[1,30,30,64]{3,1,2,0:T(8,128)} %copy.183, f32[25,30,64]{2,1,0:T(8,128)S(1)} %multiply_multiply_fusion), kind=kOutput, calls=%fused_computation.35 | convolution fusion | flops 31785600 | bytes 779400 | tf_op jit(solution)/shard_map/iqhd,ikhd->ihqk/dot_general | solution.py:98
  224.8 3.8 %fusion.13 = bf16[1,25,30,64]{3,1,2,0:T(8,128)(2,1)} fusion(bf16[1,25,30,64]{3,1,2,0:T(8,128)(2,1)} %copy.180, bf16[1,30,30,64]{3,1,2,0:T(8,128)(2,1)} %copy.179, f32[30,25]{1,0:T(8,128)S(1)} %fusion.77, f32[30,25,55]{2,1,0:T(8,128)} %copy-done.5), kind=kOutput, calls=%fused_computation.20 | convolution fusion | flops 5874954 | bytes 475200 | tf_op jit(solution)/shard_map/ihqk,ikhd->iqhd/dot_general | solution.py:102
  228.6 1.7 copy.185
  231.5 16.2 %all_gather.19 = bf16[8,25,1920]{2,1,0:T(8,128)(2,1)S(1)} all-gather(bf16[1,25,1920]{2,1,0:T(8,128)(2,1)S(1)} %convert_element_type.289), channel_id=1, replica_groups=mesh['section'=4,'tp'=8] {'tp'}, dimensions={0}, use_global_device_ids=true | all-gather | bytes 864000 | tf_op jit(solution)/shard_map/all_gather | solution.py:110
  247.7 2.3 convolution_convert_fusion.4
  250.0 4.0 %all-to-all-start.4 = ((bf16[8,25,240]{2,1,0:T(8,128)(2,1)}), bf16[8,25,240]{2,1,0:T(8,128)(2,1)}, u32[]{:S(2)}, u32[]{:S(2)}) async-start(bf16[8,25,240]{2,1,0:T(8,128)(2,1)} %convolution_convert_fusion.4), calls=%async_computation.4 | async-start | bytes 262144 | tf_op jit(solution)/shard_map/all_to_all | solution.py:193
  254.7 6.1 %all-to-all-done.4 = bf16[8,25,240]{2,1,0:T(8,128)(2,1)} async-done(((bf16[8,25,240]{2,1,0:T(8,128)(2,1)}), bf16[8,25,240]{2,1,0:T(8,128)(2,1)}, u32[]{:S(2)}, u32[]{:S(2)}) %all-to-all-start.4) | async-done | bytes 96032 | tf_op jit(solution)/shard_map/all_to_all | solution.py:193
  (177 shorter events, 65.5 us)
Async XLA Ops:
  0.0 63.4 %copy-start = (bf16[1,1920,3,240]{1,3,2,0:T(8,128)(2,1)S(1)}, bf16[1,1920,3,240]{1,3,2,0:T(8,128)(2,1)}, u32[]{:S(2)}) copy-start(bf16[1,1920,3,240]{1,3,2,0:T(8,128)(2,1)} %param.23) | copy-start | bytes 8294404
  2.2 28.1 %copy-start.3 = (bf16[1,1,25,1920]{3,2,1,0:T(8,128)(2,1)S(1)}, bf16[1,1,25,1920]{3,2,1,0:T(8,128)(2,1)}, u32[]{:S(2)}) copy-start(bf16[1,1,25,1920]{3,2,1,0:T(8,128)(2,1)} %param.14) | copy-start | bytes 288004
  4.1 27.1 %copy-start.7 = (bf16[1,2,1,30,1920]{4,1,3,2,0:T(2,128)(2,1)S(1)}, bf16[1,2,1,30,1920]{4,1,3,2,0:T(2,128)(2,1)}, u32[]{:S(2)}) copy-start(bf16[1,2,1,30,1920]{4,1,3,2,0:T(2,128)(2,1)} %param.26) | copy-start | bytes 691204
  20.8 13.9 %copy-start.8 = (bf16[1,2,1,30,1920]{4,1,3,2,0:T(2,128)(2,1)S(1)}, bf16[1,2,1,30,1920]{4,1,3,2,0:T(2,128)(2,1)}, u32[]{:S(2)}) copy-start(bf16[1,2,1,30,1920]{4,1,3,2,0:T(2,128)(2,1)} %param.27) | copy-start | bytes 691204
  25.1 18.9 %all-to-all-start = ((f32[1,2,8,3,240]{4,1,3,0,2:T(2,128)}), f32[1,2,8,3,240]{4,1,3,0,2:T(2,128)}, u32[]{:S(2)}, u32[]{:S(2)}) async-start(f32[1,2,8,3,240]{4,1,3,0,2:T(2,128)} %copy.157), calls=%async_computation | async-start | bytes 98304 | tf_op jit(solution)/shard_map/all_to_all | solution.py:158
  30.4 2.7 %copy-start.20 = (f32[25]{0:T(128)}, f32[25]{0:T(128)S(1)}, u32[]{:S(2)}) copy-start(f32[25]{0:T(128)S(1)} %broadcast_multiply_fusion.4) | copy-start | bytes 304
  38.5 4.7 %copy-start.10 = (f32[5,5,3,3]{1,0,3,2:T(8,128)S(1)}, f32[5,5,3,3]{1,0,3,2:T(8,128)}, u32[]{:S(2)}) copy-start(f32[5,5,3,3]{1,0,3,2:T(8,128)} %broadcast_multiply_fusion.1) | copy-start | bytes 2704
  45.6 91.9 %copy-start.12 = (f32[1920]{0:T(1024)}, f32[1920]{0:T(1024)S(1)}, u32[]{:S(2)}) copy-start(f32[1920]{0:T(1024)S(1)} %get-tuple-element.12) | copy-start | bytes 23044
  68.6 17.7 %all-to-all-start.1 = ((bf16[8,1,25,3,240]{4,2,3,1,0:T(8,128)(2,1)}), bf16[8,1,25,3,240]{4,2,3,1,0:T(8,128)(2,1)S(1)}, u32[]{:S(2)}, u32[]{:S(2)}) async-start(bf16[8,1,25,3,240]{4,2,3,1,0:T(8,128)(2,1)} %copy.160), calls=%async_computation.1 | async-start | bytes 786432 | tf_op jit(solution)/shard_map/all_to_all | solution.py:75
  79.9 16.9 %copy-start.21 = (f32[30]{0:T(128)}, f32[30]{0:T(128)S(1)}, u32[]{:S(2)}) copy-start(f32[30]{0:T(128)S(1)} %exponential_bitcast_fusion) | copy-start | bytes 364
  87.0 8.1 %copy-start.1 = (bf16[1,25,3,1920]{3,1,2,0:T(8,128)(2,1)}, bf16[1,25,3,1920]{3,1,2,0:T(8,128)(2,1)S(1)}, u32[]{:S(2)}) copy-start(bf16[1,25,3,1920]{3,1,2,0:T(8,128)(2,1)S(1)} %reshape.1149) | copy-start | bytes 864004
  95.7 5.3 %slice-start = ((bf16[1,25,3,1920]{3,1,2,0:T(8,128)(2,1)}), bf16[1,25,1,1920]{3,1,2,0:T(8,128)(2,1)S(1)}, s32[]{:S(2)}) async-start(bf16[1,25,3,1920]{3,1,2,0:T(8,128)(2,1)} %copy-done.1), calls=%async_computation.5 | async-start | bytes 245760 | tf_op jit(solution)/shard_map/slice | solution.py:83
  107.1 23.4 %copy-start.14 = (f32[30,32]{1,0:T(8,128)S(1)}, f32[30,32]{1,0:T(8,128)}, u32[]{:S(2)}) copy-start(f32[30,32]{1,0:T(8,128)} %gather_fusion.1) | copy-start | bytes 11524
  107.1 23.4 %copy-start.15 = (f32[25,9]{1,0:T(8,128)S(1)}, f32[25,9]{1,0:T(8,128)}, u32[]{:S(2)}) copy-start(f32[25,9]{1,0:T(8,128)} %copy.174) | copy-start | bytes 2704
  107.1 23.4 %copy-start.16 = (f32[25,4]{1,0:T(8,128)S(1)}, f32[25,4]{1,0:T(8,128)}, u32[]{:S(2)}) copy-start(f32[25,4]{1,0:T(8,128)} %copy.173) | copy-start | bytes 1204
  107.1 23.4 %copy-start.17 = (f32[25,1]{1,0:T(8,128)S(1)}, f32[25,1]{1,0:T(8,128)}, u32[]{:S(2)}) copy-start(f32[25,1]{1,0:T(8,128)} %copy.172) | copy-start | bytes 304
  107.1 23.4 %copy-start.18 = (f32[25,16]{1,0:T(8,128)S(1)}, f32[25,16]{1,0:T(8,128)}, u32[]{:S(2)}) copy-start(f32[25,16]{1,0:T(8,128)} %mul.419) | copy-start | bytes 4804
  107.2 30.4 %copy-start.4 = (bf16[1,1,25,1920]{3,2,1,0:T(8,128)(2,1)S(1)}, bf16[1,1,25,1920]{3,2,1,0:T(8,128)(2,1)}, u32[]{:S(2)}) copy-start(bf16[1,1,25,1920]{3,2,1,0:T(8,128)(2,1)} %param.14) | copy-start | bytes 288004
  108.3 32.7 %copy-start.11 = (f32[1,3,1920]{2,0,1:T(1,128)S(1)}, f32[1,3,1920]{2,0,1:T(1,128)}, u32[]{:S(2)}) copy-start(f32[1,3,1920]{2,0,1:T(1,128)} %get-tuple-element.37) | copy-start | bytes 69124
  127.1 10.1 %all-to-all-start.2 = ((bf16[8,25,240]{2,1,0:T(8,128)(2,1)}), bf16[8,25,240]{2,1,0:T(8,128)(2,1)S(1)}, u32[]{:S(2)}, u32[]{:S(2)}) async-start(bf16[8,25,240]{2,1,0:T(8,128)(2,1)} %convolution_convert_fusion.5), calls=%async_computation.2 | async-start | bytes 262144 | tf_op jit(solution)/shard_map/all_to_all | solution.py:193
  137.6 7.7 %collective-permute-start = (bf16[1,25,1920]{2,1,0:T(8,128)(2,1)S(1)}, bf16[1,25,1920]{2,1,0:T(8,128)(2,1)S(1)}, u32[]{:S(2)}, u32[]{:S(2)}) collective-permute-start(bf16[1,25,1920]{2,1,0:T(8,128)(2,1)S(1)} %fusion.44), channel_id=1, source_target_pairs={{0,8},{8,16},{16,24},{1,9},{9,17},{17,25},{2,10},{10,18},{18,26},{... | collective-permute-start | bytes 288008 | tf_op jit(solution)/shard_map/ppermute | solution.py:15
  164.3 31.8 %copy-start.9 = (bf16[30,1920]{1,0:T(8,128)(2,1)S(1)}, bf16[30,1920]{1,0:T(8,128)(2,1)}, u32[]{:S(2)}) copy-start(bf16[30,1920]{1,0:T(8,128)(2,1)} %get-tuple-element.7) | copy-start | bytes 345604
  187.7 16.6 %all-to-all-start.3 = ((bf16[8,1,25,3,240]{4,2,3,1,0:T(8,128)(2,1)}), bf16[8,1,25,3,240]{4,2,3,1,0:T(8,128)(2,1)}, u32[]{:S(2)}, u32[]{:S(2)}) async-start(bf16[8,1,25,3,240]{4,2,3,1,0:T(8,128)(2,1)} %copy.177), calls=%async_computation.3 | async-start | bytes 786432 | tf_op jit(solution)/shard_map/all_to_all | solution.py:75
  207.7 9.7 %copy-start.2 = (bf16[1,25,3,1920]{3,1,2,0:T(8,128)(2,1)}, bf16[1,25,3,1920]{3,1,2,0:T(8,128)(2,1)S(1)}, u32[]{:S(2)}) copy-start(bf16[1,25,3,1920]{3,1,2,0:T(8,128)(2,1)S(1)} %reshape.1155) | copy-start | bytes 864004
  207.8 11.1 %copy-start.22 = (f32[30]{0:T(128)S(1)}, f32[30]{0:T(128)}, u32[]{:S(2)}) copy-start(f32[30]{0:T(128)} %copy-done.21) | copy-start | bytes 364
  217.4 6.4 %slice-start.1 = ((bf16[1,25,3,1920]{3,1,2,0:T(8,128)(2,1)}), bf16[1,25,1,1920]{3,1,2,0:T(8,128)(2,1)S(1)}, s32[]{:S(2)}) async-start(bf16[1,25,3,1920]{3,1,2,0:T(8,128)(2,1)} %copy-done.2), calls=%async_computation.6 | async-start | bytes 245760 | tf_op jit(solution)/shard_map/slice | solution.py:83
  222.7 0.8 copy-start.5
  228.6 25.4 %copy-start.6 = (f32[1,1,25,1920]{3,2,1,0:T(8,128)S(1)}, f32[1,1,25,1920]{3,2,1,0:T(8,128)}, u32[]{:S(2)}) copy-start(f32[1,1,25,1920]{3,2,1,0:T(8,128)} %reshape.1190) | copy-start | bytes 576004
  228.6 25.4 %copy-start.13 = (f32[1920]{0:T(1024)S(1)}, f32[1920]{0:T(1024)}, u32[]{:S(2)}) copy-start(f32[1920]{0:T(1024)} %copy-done.12) | copy-start | bytes 23044
  230.4 33.2 %copy-start.19 = (f32[1920]{0:T(1024)S(1)}, f32[1920]{0:T(1024)}, u32[]{:S(2)}) copy-start(f32[1920]{0:T(1024)} %get-tuple-element.9) | copy-start | bytes 23044
  250.0 10.8 %all-to-all-start.4 = ((bf16[8,25,240]{2,1,0:T(8,128)(2,1)}), bf16[8,25,240]{2,1,0:T(8,128)(2,1)}, u32[]{:S(2)}, u32[]{:S(2)}) async-start(bf16[8,25,240]{2,1,0:T(8,128)(2,1)} %convolution_convert_fusion.4), calls=%async_computation.4 | async-start | bytes 262144 | tf_op jit(solution)/shard_map/all_to_all | solution.py:193
